TPU v7x, 32 devices: a whole 2x2x4 slice. The times are simulated.
32 devices in a mesh: groups: 2 (over y), px: 16 (over z, x, core).
Axes of the slice: x: 2, y: 2, z: 4, core: 2. Of those that a mesh axis runs over, the one named last changes fastest.
Arguments:
- features: bfloat16 [32, 256, 256, 256], P(None, ('groups', 'px')), parts along dimension 1, may hold values from -6 to 6
- pointwise_weight: bfloat16 [32, 32], replicated, may hold values from -1 to 1
- pointwise_bias: float32 [32], replicated, may hold values from -3 to 3
- spectral_weight: float32 [2, 32, 32, 16384], P(None, None, None, 'px'), may hold values from -6 to 6
Outputs:
- updated: bfloat16 [32, 256, 256, 256], P(None, ('groups', 'px')), parts along dimension 1
There are 2 independent parts, one for each index of `groups`. A program takes and returns all parts, laid end to end along the dimension named above; an argument that names none is the same for every part. Nothing has to cross between parts.
All inputs are finite; a program needn't handle non-finite values.
Results may differ from a plain program's by a relative error of at most 0.0025.
Values sent between devices are 32-bit elements; how exact they have to be, the bound alone decides.
No kernel may reach another device: no remote copies, remote signals or barrier semaphores. Data moves between devices by JAX's collectives and lax.ppermute only.
A program may use at most 256 MiB of HBM per device.

v0:
```python
import functools
import math

import jax
import jax.numpy as jnp
import numpy as np
from jax import lax
from jax.experimental import pallas as pl
from jax.experimental.pallas import tpu as pltpu
from jax.sharding import PartitionSpec as P

KX = 32
KY = 32
KZ = 16
TWO_PI = 2.0 * math.pi
PACK = 8
F32 = jnp.float32
BF16 = jnp.bfloat16


def np_modes(number):
    ladder = np.arange(number)
    return np.where(ladder < number // 2, ladder, ladder - number)


def np_phase(positions, frequency, length):
    product = (positions[:, None] * frequency[None, :]) % length
    return product.astype(np.float64) * (TWO_PI / length)


def split_np(table):
    table = np.asarray(table, np.float32)
    high = table.astype(jnp.bfloat16)
    low = (table - high.astype(np.float32)).astype(jnp.bfloat16)
    return high, low


def split(value):
    high = value.astype(BF16)
    low = (value - high.astype(F32)).astype(BF16)
    return high, low


def dot(left, right):
    return jnp.dot(left, right, preferred_element_type=F32)


def lane_tiles(table):
    rows, lanes = table.shape
    pad = -lanes % 128
    table = np.pad(table, ((0, 0), (0, pad)))
    return np.ascontiguousarray(table.reshape(rows, -1, 128).transpose(1, 0, 2))


def wide(ref, rows=None):
    at = slice(None) if rows is None else rows
    return jnp.concatenate([ref[i, at, :] for i in range(ref.shape[0])], axis=1)


def tile_view(array):
    *lead, length_y, length_z = array.shape
    array = array.reshape(*lead, length_y // 8, 8, length_z // 128, 128)
    return jnp.swapaxes(array, -3, -2).reshape(*lead, length_y // 8, length_z // 16, 128)


def from_tile_view(array):
    *lead, blocks, rows, _ = array.shape
    array = array.reshape(*lead, blocks, rows // 8, 8, 128)
    return jnp.swapaxes(array, -3, -2).reshape(*lead, blocks * 8, rows * 16)


def rows_of(tiles):
    count, height, _ = tiles.shape
    tiles = tiles.astype(F32).reshape(count, height // 8, 8, 128)
    return jnp.concatenate([tiles[:, t].reshape(count * 8, 128) for t in range(height // 8)], axis=1)


def forward_tables(length_y, length_z):
    z_phase = np_phase(np.arange(length_z), np.arange(KZ), length_z)
    lanes = PACK * KZ
    z_tables = np.zeros((PACK, length_z, 2 * lanes), np.float32)
    for j in range(PACK):
        z_tables[j, :, j * KZ : (j + 1) * KZ] = np.cos(z_phase)
        z_tables[j, :, lanes + j * KZ : lanes + (j + 1) * KZ] = -np.sin(z_phase)
    y_phase = np_phase(np.arange(length_y), np_modes(KY), length_y).T
    high, low = split_np(np.concatenate([np.cos(y_phase), np.sin(y_phase)], axis=0))
    z_tables = z_tables.astype(jnp.bfloat16).astype(np.float32)
    return z_tables, lane_tiles(np.concatenate([high, low], axis=0))


def forward_body(rows, block_planes, feat_ref, z_ref, y_ref, out_ref):
    plane_at, group_at = pl.program_id(0), pl.program_id(1)
    groups = pl.num_programs(1)
    blocks, height = feat_ref.shape[2:4]
    length_y = blocks * 8
    lanes = PACK * KZ
    y_table = wide(y_ref)
    total = None
    for j in range(PACK):
        part = dot(rows_of(feat_ref[j].reshape(block_planes * blocks, height, 128)), z_ref[j])
        total = part if total is None else total + part
    for p in range(block_planes):
        high, low = split(total[p * length_y : (p + 1) * length_y])
        first = dot(y_table, high)
        both = first[: 2 * KY] + first[2 * KY :] + dot(y_table[: 2 * KY], low)
        cosine, sine = both[:KY], both[KY:]
        row = group_at * rows + (plane_at * block_planes + p) * 2
        out_ref[pl.ds(row, KY, stride=groups * rows), :] = cosine[:, :lanes] + sine[:, lanes:]
        out_ref[pl.ds(row + 1, KY, stride=groups * rows), :] = cosine[:, lanes:] - sine[:, :lanes]


def forward(features, block_planes):
    channels, planes, length_y, length_z = features.shape
    groups = channels // PACK
    rows = 2 * planes
    lanes = PACK * KZ
    z_tables, y_tables = forward_tables(length_y, length_z)
    tiles = tile_view(features)
    return pl.pallas_call(
        functools.partial(forward_body, rows, block_planes),
        out_shape=jax.ShapeDtypeStruct((KY * groups * rows, lanes), F32),
        grid=(planes // block_planes, groups),
        in_specs=[
            pl.BlockSpec((PACK, block_planes) + tiles.shape[2:], lambda p, g: (g, p, 0, 0, 0)),
            pl.BlockSpec(z_tables.shape, lambda p, g: (0, 0, 0)),
            pl.BlockSpec(y_tables.shape, lambda p, g: (0, 0, 0)),
        ],
        out_specs=pl.BlockSpec((KY * groups * rows, lanes), lambda p, g: (0, 0)),
        compiler_params=pltpu.CompilerParams(
            dimension_semantics=("arbitrary", "arbitrary"), vmem_limit_bytes=40 << 20
        ),
        name="forward_zy",
    )(tiles, jnp.asarray(z_tables), jnp.asarray(y_tables))


def middle_tables(length_x):
    phase = np_phase(np.arange(length_x), np_modes(KX), length_x)
    cosine, sine = np.cos(phase), np.sin(phase)
    ahead = np.zeros((2, KX, length_x, 2), np.float32)
    ahead[0, :, :, 0], ahead[0, :, :, 1] = cosine.T, sine.T
    ahead[1, :, :, 0], ahead[1, :, :, 1] = -sine.T, cosine.T
    high, low = split_np(ahead.reshape(2 * KX, 2 * length_x))
    back = np.zeros((length_x, 2, 2, KX), np.float32)
    back[:, 0, 0], back[:, 0, 1] = cosine, -sine
    back[:, 1, 0], back[:, 1, 1] = sine, cosine
    back_high, back_low = split_np(back.reshape(2 * length_x, 2 * KX))
    return (
        lane_tiles(np.concatenate([high, low], axis=0)),
        lane_tiles(np.concatenate([back_high, back_high, back_low], axis=1)),
    )


def regroup(pieces):
    count = len(pieces)
    width = pieces[0].shape[-1] // count
    group = lax.broadcasted_iota(jnp.int32, pieces[0].shape, 1) // width
    results = []
    for a in range(count):
        value = None
        for b in range(count):
            shift = ((b - a) * width) % (count * width)
            moved = pltpu.roll(pieces[b], shift, axis=1) if shift else pieces[b]
            value = moved if value is None else jnp.where(group == b, moved, value)
        results.append(value)
    return results


def middle_body(local, groups, in_ref, weight_ref, ahead_ref, back_ref, out_ref, turned, spec, mixed):
    devices, _, lanes = in_ref.shape
    rows = in_ref.shape[1] // (local * groups)
    channels = groups * PACK
    quarter = KZ // 4
    tables = wide(ahead_ref)
    back_table = wide(back_ref)[:, : 6 * KX]
    for g in range(groups):
        found = []
        for k in range(local):
            at = (k * groups + g) * rows
            high, low = split(in_ref[:, at : at + rows, :].reshape(devices * rows, lanes))
            first = dot(tables, high)
            found.append(first[: 2 * KX] + first[2 * KX :] + dot(tables[: 2 * KX], low))
        turned[...] = jnp.concatenate(found, axis=0).T
        for t in range(quarter):
            pieces = [turned[pl.ds(4 * t + j, PACK, stride=KZ), :] for j in range(4)]
            for a, value in enumerate(regroup(pieces)):
                k, r = a // 2, a % 2
                spec[r, g * PACK : (g + 1) * PACK, (k * quarter + t) * 128 : (k * quarter + t + 1) * 128] = value

    def mix(tile, carry):
        here = pl.ds(pl.multiple_of(tile * 128, 128), 128)
        real = imag = None
        for i in range(channels):
            s_real, s_imag = spec[0, i : i + 1, here], spec[1, i : i + 1, here]
            w_real, w_imag = weight_ref[0, i, :, here], weight_ref[1, i, :, here]
            add_real = s_real * w_real - s_imag * w_imag
            add_imag = s_real * w_imag + s_imag * w_real
            real = add_real if real is None else real + add_real
            imag = add_imag if imag is None else imag + add_imag
        mixed[0, :, here] = real
        mixed[1, :, here] = imag
        return carry

    lax.fori_loop(0, local * quarter, mix, 0)
    for g in range(groups):
        for t in range(quarter):
            pieces = [
                mixed[a % 2, g * PACK : (g + 1) * PACK, ((a // 2) * quarter + t) * 128 : ((a // 2) * quarter + t + 1) * 128]
                for a in range(4)
            ]
            for j, value in enumerate(regroup(pieces)):
                turned[pl.ds(4 * t + j, PACK, stride=KZ), :] = value
        modes = turned[...].T
        for k in range(local):
            high, low = split(modes[k * 2 * KX : (k + 1) * 2 * KX])
            spread = dot(back_table, jnp.concatenate([high, low, high], axis=0))
            at = (k * groups + g) * rows
            out_ref[:, at : at + rows, :] = spread.reshape(devices, rows, lanes)


def middle(gathered, spectral_weight, length_x, local, groups):
    channels = spectral_weight.shape[1]
    ahead, back = middle_tables(length_x)
    modes = spectral_weight.shape[3]
    whole = pl.BlockSpec(memory_space=pltpu.VMEM)
    return pl.pallas_call(
        functools.partial(middle_body, local, groups),
        out_shape=jax.ShapeDtypeStruct(gathered.shape, F32),
        in_specs=[whole] * 4,
        out_specs=whole,
        scratch_shapes=[
            pltpu.VMEM((PACK * KZ, local * 2 * KX), F32),
            pltpu.VMEM((2, channels, modes), F32),
            pltpu.VMEM((2, channels, modes), F32),
        ],
        compiler_params=pltpu.CompilerParams(vmem_limit_bytes=32 << 20),
        name="middle_x",
    )(gathered, spectral_weight, jnp.asarray(ahead), jnp.asarray(back))


def final_tables(length_x, length_y, length_z):
    y_phase = np_phase(np.arange(length_y), np_modes(KY), length_y)
    high, low = split_np(np.concatenate([np.cos(y_phase), np.sin(y_phase)], axis=1))
    y_table = np.concatenate([high, high, low], axis=1)
    z_phase = np_phase(np.arange(length_z), np.arange(KZ), length_z).T
    factor = np.where(np.arange(KZ) == 0, 1.0, 2.0)[:, None] * (0.5 / (1.0 * length_x * length_y * length_z))
    z_high, z_low = split_np(np.concatenate([factor * np.cos(z_phase), -factor * np.sin(z_phase)], axis=0))
    ones = np.zeros((2 * KZ, length_z), np.float32)
    ones[:3] = 1.0
    z_table = np.concatenate([z_high, z_high, z_low, ones.astype(jnp.bfloat16)], axis=0)
    lanes = PACK * KZ
    pick = np.zeros((2, lanes, 2, PACK, 4, 2, KZ), np.float32)
    kz = np.arange(KZ)
    for o in range(PACK):
        for copy in range(4):
            pick[0, o * KZ + kz, 0, o, copy, 0, kz] = 1.0
            pick[1, o * KZ + kz, 0, o, copy, 1, kz] = 1.0
            pick[1, o * KZ + kz, 1, o, copy, 0, kz] = -1.0
            pick[0, o * KZ + kz, 1, o, copy, 1, kz] = 1.0
    pick = pick.reshape(2 * lanes, 2 * PACK * lanes).astype(jnp.bfloat16)
    return lane_tiles(y_table), lane_tiles(z_table), lane_tiles(pick)


def final_body(rows, chunk, modes_ref, feat_ref, kron_ref, bias_ref, y_ref, z_ref, pick_ref, out_ref, picked, half):
    plane, part_at = pl.program_id(0), pl.program_id(1)
    channels = feat_ref.shape[0]
    groups = channels // PACK
    length_y = y_ref.shape[1]
    length_z = feat_ref.shape[3] * 16
    lanes = PACK * KZ

    @pl.when(part_at == 0)
    def prepare():
        stacked = []
        for g in range(groups):
            row = g * rows + plane * 2
            real = modes_ref[pl.ds(row, KY, stride=groups * rows), :]
            imag = modes_ref[pl.ds(row + 1, KY, stride=groups * rows), :]
            high, low = split(jnp.concatenate([real, imag], axis=1))
            stacked += [high, low]
        left = jnp.concatenate(stacked, axis=0)
        for at in range(0, 2 * PACK, 2):
            value = dot(left, jnp.concatenate([pick_ref[at], pick_ref[at + 1]], axis=1)).astype(BF16)
            picked[at] = value[:, :lanes]
            picked[at + 1] = value[:, lanes:]
        y_table = wide(y_ref)[:, : 6 * KY]
        lane = lax.broadcasted_iota(jnp.int32, (length_y // 8, 16, lanes), 2)
        for g in range(groups):
            high, low = 2 * g * KY, (2 * g + 1) * KY
            for pair in range(PACK // 2):
                parts = [
                    jnp.concatenate(
                        [picked[s * PACK + 2 * pair + i, h : h + KY, :] for h in (high, low, high) for s in range(2)],
                        axis=0,
                    )
                    for i in range(2)
                ]
                found = dot(y_table, jnp.concatenate(parts, axis=1))
                found = found.reshape(length_y // 8, 8, 2 * lanes)
                found = jnp.concatenate([found[:, :, :lanes], found[:, :, lanes:]], axis=1)
                top = found.astype(BF16)
                rest = (found - top.astype(F32)).astype(BF16)
                value = jnp.where(lane // (2 * KZ) == 1, rest, top)
                first = (g * PACK + 2 * pair) * 8
                value = jnp.where(lane < 6 * KZ, value, bias_ref[first : first + 16, :][None])
                half[:, first : first + 16, :] = value

    def block(b, carry):
        feats = rows_of(feat_ref[:, 0, b])
        h = dot(kron_ref[...], feats) + dot(half[part_at * (chunk // 8) + b], wide(z_ref))
        inner = h * (h * h * (8.0 * 0.7978845608 * 0.044715) + 2.0 * 0.7978845608)
        result = h * jnp.tanh(inner) + h
        result = result.reshape(channels, 8, length_z)
        parts = [result[:, :, t * 128 : (t + 1) * 128] for t in range(length_z // 128)]
        out_ref[:, 0, b] = jnp.concatenate(parts, axis=1).astype(BF16)
        return carry

    lax.fori_loop(0, chunk // 8, block, 0, unroll=8)


def final(spread, features, pointwise_weight, pointwise_bias, length_x, chunk):
    channels, planes, length_y, length_z = features.shape
    rows = 2 * planes
    groups = channels // PACK
    lanes = PACK * KZ
    y_table, z_table, pick = final_tables(length_x, length_y, length_z)
    kron = jnp.kron(0.5 * pointwise_weight.astype(F32), jnp.eye(8, dtype=F32))
    tiles = tile_view(features)
    bias = 0.5 * pointwise_bias
    b0 = lax.reduce_precision(bias, 8, 7)
    b1 = lax.reduce_precision(bias - b0, 8, 7)
    b2 = bias - b0 - b1
    pieces = jnp.stack([b0, b1, b2], axis=1)
    bias_rows = jnp.pad(pieces, ((0, 0), (6 * KZ, lanes - 6 * KZ - 3))).astype(BF16)
    bias_rows = jnp.repeat(bias_rows, 8, axis=0)

    def fixed(array):
        return pl.BlockSpec(array.shape, lambda p, q: (0,) * array.ndim)

    tables = [jnp.asarray(y_table), jnp.asarray(z_table), jnp.asarray(pick)]
    grid_block = pl.BlockSpec((channels, 1, chunk // 8, tiles.shape[3], 128), lambda p, q: (0, p, q, 0, 0))
    out = pl.pallas_call(
        functools.partial(final_body, rows, chunk),
        out_shape=jax.ShapeDtypeStruct(tiles.shape, BF16),
        grid=(planes, length_y // chunk),
        in_specs=[fixed(spread), grid_block, fixed(kron), fixed(bias_rows)] + [fixed(t) for t in tables],
        out_specs=grid_block,
        scratch_shapes=[
            pltpu.VMEM((2 * PACK, groups * 2 * KY, lanes), BF16),
            pltpu.VMEM((length_y // 8, channels * 8, lanes), BF16),
        ],
        compiler_params=pltpu.CompilerParams(
            dimension_semantics=("arbitrary", "arbitrary"), vmem_limit_bytes=48 << 20
        ),
        name="final_yz",
    )(spread, tiles, kron, bias_rows, *tables)
    return from_tile_view(out)


def fused(devices, features, pointwise_weight, pointwise_bias, spectral_weight):
    channels, planes = features.shape[:2]
    length_x = planes * devices
    local = KY // devices
    groups = channels // PACK
    rows = 2 * planes
    lanes = PACK * KZ
    shape = (devices, local * groups * rows, lanes)
    partial_value = forward(features, 4).reshape(shape)
    gathered = lax.all_to_all(partial_value, "px", split_axis=0, concat_axis=0)
    spread = middle(gathered, spectral_weight, length_x, local, groups)
    spread = lax.all_to_all(spread, "px", split_axis=0, concat_axis=0)
    spread = spread.reshape(KY * groups * rows, lanes)
    return final(spread, features, pointwise_weight, pointwise_bias, length_x, 128)


def signed_modes(number):
    ladder = jnp.arange(number, dtype=jnp.int32)
    return jnp.where(ladder < number // 2, ladder, ladder - number)


def phase_table(positions, frequency, length):
    product = positions[:, None] * frequency[None, :] % length
    return product.astype(jnp.float32) * (TWO_PI / length)


def forward_table(positions):
    x_phase = phase_table(positions, signed_modes(KX), positions.shape[0])
    cosine = jnp.cos(x_phase)
    sine = jnp.sin(x_phase)
    return jnp.stack(
        [jnp.stack([cosine, -sine], axis=1), jnp.stack([sine, cosine], axis=1)], axis=0
    )


def inverse_table(positions):
    x_phase = phase_table(positions, signed_modes(KX), positions.shape[0])
    cosine = jnp.cos(x_phase)
    sine = jnp.sin(x_phase)
    return jnp.stack(
        [jnp.stack([cosine, sine], axis=1), jnp.stack([-sine, cosine], axis=1)], axis=0
    )


def spectra_local(features):
    channels, planes, Y, Z = features.shape
    z_phase = phase_table(jnp.arange(Z, dtype=jnp.int32), jnp.arange(KZ, dtype=jnp.int32), Z)
    z_table = jnp.concatenate([jnp.cos(z_phase), -jnp.sin(z_phase)], axis=1).astype(jnp.bfloat16)
    flat = features.reshape(channels * planes * Y, Z)
    along_z = jnp.dot(flat, z_table, preferred_element_type=jnp.float32)
    stacked = along_z.reshape(channels, planes, Y, 2, KZ).transpose(3, 0, 1, 4, 2)
    y_phase = phase_table(jnp.arange(Y, dtype=jnp.int32), signed_modes(KY), Y)
    cosine = jnp.einsum(
        "rcxky,yj->rcxjk", stacked, jnp.cos(y_phase), precision=lax.Precision.HIGHEST
    )
    sine = jnp.einsum("rcxky,yj->rcxjk", stacked, jnp.sin(y_phase), precision=lax.Precision.HIGHEST)
    real_part = cosine[0] + sine[1]
    imag_part = cosine[1] - sine[0]
    return jnp.stack([real_part, imag_part]).reshape(2, channels, planes, KY * KZ)


def along_first(partial_value, table):
    return jnp.einsum("rcxq,rxsk->qsck", partial_value, table, precision=lax.Precision.HIGHEST)


def contract(left, right):
    return jnp.einsum("im,iom->om", left, right, precision=lax.Precision.HIGHEST)


def mix_modes(spectrum, weights):
    real_part = contract(spectrum[0], weights[0]) - contract(spectrum[1], weights[1])
    imag_part = contract(spectrum[0], weights[1]) + contract(spectrum[1], weights[0])
    return jnp.stack([real_part, imag_part])


def back_first(blended, table):
    return jnp.einsum("rcqk,rxsk->scxq", blended, table, precision=lax.Precision.HIGHEST)


def finish_planes(length_x, spread, features, pointwise_weight, pointwise_bias):
    channels, planes, Y, Z = features.shape
    X = length_x
    folded = spread.reshape(2, channels, planes, KY, KZ)
    y_phase = phase_table(jnp.arange(Y, dtype=jnp.int32), signed_modes(KY), Y)
    cosine = jnp.einsum(
        "rcxjk,yj->rcxky", folded, jnp.cos(y_phase), precision=lax.Precision.HIGHEST
    )
    sine = jnp.einsum("rcxjk,yj->rcxky", folded, jnp.sin(y_phase), precision=lax.Precision.HIGHEST)
    halves = jnp.concatenate([cosine[0] - sine[1], sine[0] + cosine[1]], axis=2)
    z_phase = phase_table(jnp.arange(Z, dtype=jnp.int32), jnp.arange(KZ, dtype=jnp.int32), Z)
    factor = jnp.where(jnp.arange(KZ, dtype=jnp.int32) == 0, 1.0, 2.0).astype(jnp.float32) / (
        1.0 * X * Y * Z
    )
    z_table = jnp.concatenate(
        [factor[:, None] * jnp.cos(z_phase).T, -factor[:, None] * jnp.sin(z_phase).T], axis=0
    )
    spectral = jnp.einsum("cxjy,jz->cxyz", halves, z_table, precision=lax.Precision.HIGHEST)
    linear = jnp.dot(
        pointwise_weight,
        features.reshape(channels, planes * Y * Z),
        preferred_element_type=jnp.float32,
    ).reshape(channels, planes, Y, Z)
    summed = spectral + linear + pointwise_bias[:, None, None, None]
    inner = 0.7978845608 * (summed + 0.044715 * summed * summed * summed)
    return (0.5 * summed * (1.0 + jnp.tanh(inner))).astype(jnp.bfloat16)


def plain(length_x, features, pointwise_weight, pointwise_bias, spectral_weight):
    every_plane = jnp.arange(length_x, dtype=jnp.int32)
    channels = features.shape[0]
    partial_value = spectra_local(features)
    gathered = lax.all_to_all(partial_value, "px", split_axis=3, concat_axis=2, tiled=True)
    spectrum = along_first(gathered, forward_table(every_plane)).transpose(1, 2, 0, 3)
    local_pairs = spectrum.shape[2]
    blended = mix_modes(
        spectrum.reshape(2, channels, local_pairs * KX), spectral_weight
    ).reshape(
        2, channels, local_pairs, KX
    )
    spread = lax.all_to_all(
        back_first(blended, inverse_table(every_plane)),
        "px",
        split_axis=2,
        concat_axis=3,
        tiled=True,
    )
    return finish_planes(length_x, spread, features, pointwise_weight, pointwise_bias)


def on_device(devices, features, pointwise_weight, pointwise_bias, spectral_weight):
    channels, planes, length_y, length_z = features.shape
    fits = (
        KY == 2 * devices
        and planes % 4 == 0
        and channels % PACK == 0
        and length_y % 128 == 0
        and length_z % 128 == 0
    )
    call = functools.partial(fused, devices) if fits else functools.partial(plain, planes * devices)
    return call(features, pointwise_weight, pointwise_bias, spectral_weight)


def solution(mesh):
    in_specs = (P(None, ("groups", "px"), None, None), P(), P(), P(None, None, None, "px"))
    out_specs = P(None, ("groups", "px"), None, None)
    return jax.shard_map(
        functools.partial(on_device, mesh.shape["px"]),
        mesh=mesh,
        in_specs=in_specs,
        out_specs=out_specs,
        check_vma=False,
    )
```

profile of v0, /device:TPU:0, one launch (start us, length us, event | category | flops | bytes accessed | tf_op | source)
XLA Modules:
  0.0 128.5 jit_solution(16179885177671703497)
XLA Ops:
  0.0 1.7 %copy-done = f32[8,256,256]{2,1,0:T(8,128)S(1)} copy-done((f32[8,256,256]{2,1,0:T(8,128)S(1)}, f32[8,256,256]{2,1,0:T(8,128)}, u32[]{:S(2)}) %copy-start) | copy-done | bytes 2097176
  1.7 1.0 copy-done.4
  2.7 17.4 %forward_zy.1 = f32[2048,128]{1,0:T(8,128)S(1)} custom-call(bf16[32,8,32,16,128]{4,3,2,1,0:T(8,128)(2,1)} %bitcast.26, f32[8,256,256]{2,1,0:T(8,128)S(1)} %copy-done, bf16[2,128,128]{2,1,0:T(8,128)(2,1)S(1)} %copy-done.4), custom_call_target="tpu_custom_call" | custom-call | tf_op jit(solution)/shard_map/forward_zy/pallas_call | solution.py:119
  20.1 31.9 %all_to_all.10.in_ref = f32[16,128,128]{2,1,0:T(8,128)S(1)} all-to-all(f32[16,128,128]{2,1,0:T(8,128)S(1)} %bitcast.25), channel_id=1, replica_groups=mesh['groups'=2,'px'=16] {'px'}, dimensions={0} | all-to-all | bytes 2097152 | tf_op jit(solution)/shard_map/all_to_all | solution.py:368
  52.0 0.0 slice-done
  52.0 0.0 slice-done.1
  52.0 0.0 copy-done.3
  52.0 0.0 copy-done.5
  52.0 0.0 copy-start.8
  52.0 0.0 copy-start.7
  52.0 5.2 %middle_x.1 = f32[16,128,128]{2,1,0:T(8,128)} custom-call(f32[16,128,128]{2,1,0:T(8,128)S(1)} %all_to_all.10.in_ref, f32[2,32,32,1024]{3,2,1,0:T(8,128)S(1)} %bitcast.23, bf16[2,128,128]{2,1,0:T(8,128)(2,1)S(1)} %copy-done.5, bf16[2,256,128]{2,1,0:T(8,128)(2,1)S(1)} %copy-done.3), custom_call_target="tpu_custom_call" | custom-call | tf_op jit(solution)/shard_map/middle_x/pallas_call | solution.py:225
  57.2 5.0 %all-to-all-start.1 = ((f32[16,128,128]{2,1,0:T(8,128)}), f32[16,128,128]{2,1,0:T(8,128)S(1)}, u32[]{:S(2)}, u32[]{:S(2)}) async-start(f32[16,128,128]{2,1,0:T(8,128)} %middle_x.1), calls=%async_computation.1 | async-start | bytes 2097152 | tf_op jit(solution)/shard_map/all_to_all | solution.py:370
  62.2 0.0 copy-done.8
  62.2 0.1 copy.14
  62.3 0.0 copy-done.7
  62.4 0.0 copy-start.1
  62.4 0.0 copy-start.2
  62.4 0.0 copy-start.6
  62.4 2.6 %broadcast_multiply_fusion = f32[32,8,32,8]{3,2,1,0:T(8,128)} fusion(f32[8,8]{1,0:T(8,128)S(1)} %fusion, f32[32,32]{1,0:T(8,128)S(1)} %convert_multiply_fusion), kind=kLoop, calls=%fused_computation | loop fusion | flops 65536 | bytes 266496 | tf_op jit(solution)/shard_map/jit(kron)/mul | solution.py:326
  65.0 4.0 %mul.41.kron_ref = f32[256,256]{1,0:T(8,128)S(1)} reshape(f32[32,8,32,8]{3,2,1,0:T(8,128)} %broadcast_multiply_fusion) | data formatting | bytes 524288 | tf_op jit(solution)/shard_map/jit(kron)/mul | solution.py:326
  69.0 0.1 pad.5.clone
  69.1 16.0 %all-to-all-done.1 = f32[16,128,128]{2,1,0:T(8,128)S(1)} async-done(((f32[16,128,128]{2,1,0:T(8,128)}), f32[16,128,128]{2,1,0:T(8,128)S(1)}, u32[]{:S(2)}, u32[]{:S(2)}) %all-to-all-start.1) | async-done | bytes 1048608 | tf_op jit(solution)/shard_map/all_to_all | solution.py:370
  85.1 0.0 copy-done.1
  85.1 43.4 %final_yz.1 = bf16[32,8,32,16,128]{4,3,2,1,0:T(8,128)(2,1)} custom-call(f32[2048,128]{1,0:T(8,128)S(1)} %bitcast.24, bf16[32,8,32,16,128]{4,3,2,1,0:T(8,128)(2,1)} %bitcast.27, f32[256,256]{1,0:T(8,128)S(1)} %mul.41.kron_ref, bf16[256,128]{1,0:T(8,128)(2,1)S(1)} %broadcast_bitcast_fusion.bias_ref, bf16[2,256,128]{2,1,0:T(8,128)(2,1)S(1)} %copy-done.2, ...), custom_call_target="tpu_custom_call" | custom-call | tf_op jit(solution)/shard_map/final_yz/pallas_call | solution.py:341
  (14 shorter events, 0.1 us)
Async XLA Ops:
  0.0 52.0 %slice-start = ((s8[8388608]{0:T(1024)(128)(4,1)}), s8[4194304]{0:T(1024)(128)(4,1)S(1)}, s32[]{:S(2)}) async-start(s8[8388608]{0:T(1024)(128)(4,1)} %bitcast.22), calls=%async_computation.2 | async-start | bytes 8388608
  0.0 1.7 %copy-start = (f32[8,256,256]{2,1,0:T(8,128)S(1)}, f32[8,256,256]{2,1,0:T(8,128)}, u32[]{:S(2)}) copy-start(f32[8,256,256]{2,1,0:T(8,128)} %constant.21.clone.z_ref) | copy-start | bytes 6291460
  1.7 1.0 copy-start.4
  2.7 49.2 %slice-start.1 = ((s8[8388608]{0:T(1024)(128)(4,1)}), s8[4194304]{0:T(1024)(128)(4,1)S(1)}, s32[]{:S(2)}) async-start(s8[8388608]{0:T(1024)(128)(4,1)} %bitcast.22), calls=%async_computation.3 | async-start | bytes 8388608
  2.7 49.2 %copy-start.3 = (bf16[2,256,128]{2,1,0:T(8,128)(2,1)S(1)}, bf16[2,256,128]{2,1,0:T(8,128)(2,1)}, u32[]{:S(2)}) copy-start(bf16[2,256,128]{2,1,0:T(8,128)(2,1)} %constant.24.clone.back_ref) | copy-start | bytes 393220
  2.7 49.2 %copy-start.5 = (bf16[2,128,128]{2,1,0:T(8,128)(2,1)S(1)}, bf16[2,128,128]{2,1,0:T(8,128)(2,1)}, u32[]{:S(2)}) copy-start(bf16[2,128,128]{2,1,0:T(8,128)(2,1)} %constant.23.clone.ahead_ref) | copy-start | bytes 196612
  52.0 10.2 %copy-start.8 = (f32[32]{0:T(128)S(1)}, f32[32]{0:T(128)}, u32[]{:S(2)}) copy-start(f32[32]{0:T(128)} %param.13) | copy-start | bytes 388
  52.0 10.3 %copy-start.7 = (bf16[32,32]{1,0:T(8,128)(2,1)S(1)}, bf16[32,32]{1,0:T(8,128)(2,1)}, u32[]{:S(2)}) copy-start(bf16[32,32]{1,0:T(8,128)(2,1)} %param.12) | copy-start | bytes 6148
  57.2 27.9 %all-to-all-start.1 = ((f32[16,128,128]{2,1,0:T(8,128)}), f32[16,128,128]{2,1,0:T(8,128)S(1)}, u32[]{:S(2)}, u32[]{:S(2)}) async-start(f32[16,128,128]{2,1,0:T(8,128)} %middle_x.1), calls=%async_computation.1 | async-start | bytes 2097152 | tf_op jit(solution)/shard_map/all_to_all | solution.py:370
  62.4 22.7 %copy-start.1 = (bf16[16,256,128]{2,1,0:T(8,128)(2,1)S(1)}, bf16[16,256,128]{2,1,0:T(8,128)(2,1)}, u32[]{:S(2)}) copy-start(bf16[16,256,128]{2,1,0:T(8,128)(2,1)} %constant.27.clone.pick_ref) | copy-start | bytes 3145732
  62.4 22.7 %copy-start.2 = (bf16[2,256,128]{2,1,0:T(8,128)(2,1)S(1)}, bf16[2,256,128]{2,1,0:T(8,128)(2,1)}, u32[]{:S(2)}) copy-start(bf16[2,256,128]{2,1,0:T(8,128)(2,1)} %constant.25.clone.y_ref) | copy-start | bytes 393220
  62.4 22.7 %copy-start.6 = (bf16[2,128,128]{2,1,0:T(8,128)(2,1)S(1)}, bf16[2,128,128]{2,1,0:T(8,128)(2,1)}, u32[]{:S(2)}) copy-start(bf16[2,128,128]{2,1,0:T(8,128)(2,1)} %constant.26.clone.z_ref) | copy-start | bytes 196612
where the time goes:
time: 130 us; the launch traced here: 129 us
  Pallas kernels  65.9 us (51%)
  blocking collectives  31.9 us (25%)
  waiting for transfers between devices  16 us (12%)
  local copies, waits for them, and re-layouts  6.98 us (5%)
  starting transfers between devices  5.02 us (4%)
  other arithmetic  2.64 us (2%)
    pallas_call x1, Pallas kernels, final(): pl.pallas_call(functools.partial(final_body, rows, chunk), out_shape=jax....  43.4 us
    all_to_all x1, blocking collectives, fused(): gathered = lax.all_to_all(partial_value, 'px', split_axis=0, concat_axis=0)  31.9 us
    pallas_call x1, Pallas kernels, forward(): pl.pallas_call(functools.partial(forward_body, rows, block_planes), out_s...  17.4 us
    all_to_all x1, waiting for transfers between devices, fused(): spread = lax.all_to_all(spread, 'px', split_axis=0, concat_axis=0)  16 us
    pallas_call x1, Pallas kernels, middle(): pl.pallas_call(functools.partial(middle_body, local, groups), out_shape=j...  5.15 us
    all_to_all x1, starting transfers between devices, fused(): spread = lax.all_to_all(spread, 'px', split_axis=0, concat_axis=0)  5.02 us
    mul x1, local copies, waits for them, and re-layouts, final(): kron = jnp.kron(0.5 * pointwise_weight.astype(F32), jnp.eye(8, dtype=F32))  4.02 us
    unnamed x23, local copies, waits for them, and re-layouts  2.88 us
  transfers between devices with their start and end apart: 1, of which 1 were waited for; matrix products, arithmetic and copies ran while one was open for 5% of the time, Pallas kernels for 0%

commit v1 on v0

--- a/solution.py
+++ b/solution.py
@@ -13,6 +13,7 @@
 KY = 32
 KZ = 16
 TWO_PI = 2.0 * math.pi
+UNROLL = 32
 PACK = 8
 F32 = jnp.float32
 BF16 = jnp.bfloat16
@@ -84,7 +85,7 @@
         z_tables[j, :, lanes + j * KZ : lanes + (j + 1) * KZ] = -np.sin(z_phase)
     y_phase = np_phase(np.arange(length_y), np_modes(KY), length_y).T
     high, low = split_np(np.concatenate([np.cos(y_phase), np.sin(y_phase)], axis=0))
-    z_tables = z_tables.astype(jnp.bfloat16).astype(np.float32)
+    z_tables = np.stack([lane_tiles(table) for table in z_tables.astype(jnp.bfloat16)])
     return z_tables, lane_tiles(np.concatenate([high, low], axis=0))
 
 
@@ -97,7 +98,7 @@
     y_table = wide(y_ref)
     total = None
     for j in range(PACK):
-        part = dot(rows_of(feat_ref[j].reshape(block_planes * blocks, height, 128)), z_ref[j])
+        part = dot(rows_of(feat_ref[j].reshape(block_planes * blocks, height, 128)).astype(BF16), wide(z_ref.at[j]))
         total = part if total is None else total + part
     for p in range(block_planes):
         high, low = split(total[p * length_y : (p + 1) * length_y])
@@ -122,7 +123,7 @@
         grid=(planes // block_planes, groups),
         in_specs=[
             pl.BlockSpec((PACK, block_planes) + tiles.shape[2:], lambda p, g: (g, p, 0, 0, 0)),
-            pl.BlockSpec(z_tables.shape, lambda p, g: (0, 0, 0)),
+            pl.BlockSpec(z_tables.shape, lambda p, g: (0, 0, 0, 0)),
             pl.BlockSpec(y_tables.shape, lambda p, g: (0, 0, 0)),
         ],
         out_specs=pl.BlockSpec((KY * groups * rows, lanes), lambda p, g: (0, 0)),
@@ -130,7 +131,11 @@
             dimension_semantics=("arbitrary", "arbitrary"), vmem_limit_bytes=40 << 20
         ),
         name="forward_zy",
-    )(tiles, jnp.asarray(z_tables), jnp.asarray(y_tables))
+    )(
+        tiles,
+        pltpu.with_memory_space_constraint(jnp.asarray(z_tables), pltpu.HBM),
+        pltpu.with_memory_space_constraint(jnp.asarray(y_tables), pltpu.HBM),
+    )
 
 
 def middle_tables(length_x):
@@ -165,7 +170,8 @@
     return results
 
 
-def middle_body(local, groups, in_ref, weight_ref, ahead_ref, back_ref, out_ref, turned, spec, mixed):
+def middle_body(local, groups, parts, in_ref, weight_ref, ahead_ref, back_ref, *rest):
+    out_refs, (turned, spec, mixed) = rest[:parts], rest[parts:]
     devices, _, lanes = in_ref.shape
     rows = in_ref.shape[1] // (local * groups)
     channels = groups * PACK
@@ -213,20 +219,23 @@
         for k in range(local):
             high, low = split(modes[k * 2 * KX : (k + 1) * 2 * KX])
             spread = dot(back_table, jnp.concatenate([high, low, high], axis=0))
-            at = (k * groups + g) * rows
-            out_ref[:, at : at + rows, :] = spread.reshape(devices, rows, lanes)
-
-
-def middle(gathered, spectral_weight, length_x, local, groups):
+            spread = spread.reshape(devices, rows, lanes)
+            size = rows // parts
+            at = (k * groups + g) * size
+            for part, out_ref in enumerate(out_refs):
+                out_ref[:, at : at + size, :] = spread[:, part * size : (part + 1) * size]
+
+
+def middle(gathered, spectral_weight, length_x, local, groups, parts):
     channels = spectral_weight.shape[1]
     ahead, back = middle_tables(length_x)
     modes = spectral_weight.shape[3]
     whole = pl.BlockSpec(memory_space=pltpu.VMEM)
     return pl.pallas_call(
-        functools.partial(middle_body, local, groups),
-        out_shape=jax.ShapeDtypeStruct(gathered.shape, F32),
+        functools.partial(middle_body, local, groups, parts),
+        out_shape=[jax.ShapeDtypeStruct((gathered.shape[0], gathered.shape[1] // parts, gathered.shape[2]), F32)] * parts,
         in_specs=[whole] * 4,
-        out_specs=whole,
+        out_specs=[whole] * parts,
         scratch_shapes=[
             pltpu.VMEM((PACK * KZ, local * 2 * KX), F32),
             pltpu.VMEM((2, channels, modes), F32),
@@ -240,33 +249,40 @@
 def final_tables(length_x, length_y, length_z):
     y_phase = np_phase(np.arange(length_y), np_modes(KY), length_y)
     high, low = split_np(np.concatenate([np.cos(y_phase), np.sin(y_phase)], axis=1))
-    y_table = np.concatenate([high, high, low], axis=1)
+    ones = np.zeros((length_y, 16), np.float32)
+    ones[:, :3] = 1.0
+    y_table = np.concatenate([high, high, low, ones.astype(jnp.bfloat16)], axis=1)
     z_phase = np_phase(np.arange(length_z), np.arange(KZ), length_z).T
     factor = np.where(np.arange(KZ) == 0, 1.0, 2.0)[:, None] * (0.5 / (1.0 * length_x * length_y * length_z))
     z_high, z_low = split_np(np.concatenate([factor * np.cos(z_phase), -factor * np.sin(z_phase)], axis=0))
-    ones = np.zeros((2 * KZ, length_z), np.float32)
-    ones[:3] = 1.0
-    z_table = np.concatenate([z_high, z_high, z_low, ones.astype(jnp.bfloat16)], axis=0)
-    lanes = PACK * KZ
-    pick = np.zeros((2, lanes, 2, PACK, 4, 2, KZ), np.float32)
+    z_table = np.zeros((2, 256, length_z), jnp.bfloat16)
+    for slot in range(2):
+        at = slot * 64
+        z_table[slot, at : at + 32] = z_high
+        z_table[slot, at + 32 : at + 64] = z_low
+        z_table[slot, 128 + at : 128 + at + 32] = z_high
+    lanes = PACK * KZ
+    pick = np.zeros((2, lanes, 2, PACK, 2, 2, KZ), np.float32)
     kz = np.arange(KZ)
     for o in range(PACK):
-        for copy in range(4):
+        for copy in range(2):
             pick[0, o * KZ + kz, 0, o, copy, 0, kz] = 1.0
             pick[1, o * KZ + kz, 0, o, copy, 1, kz] = 1.0
             pick[1, o * KZ + kz, 1, o, copy, 0, kz] = -1.0
             pick[0, o * KZ + kz, 1, o, copy, 1, kz] = 1.0
-    pick = pick.reshape(2 * lanes, 2 * PACK * lanes).astype(jnp.bfloat16)
-    return lane_tiles(y_table), lane_tiles(z_table), lane_tiles(pick)
-
-
-def final_body(rows, chunk, modes_ref, feat_ref, kron_ref, bias_ref, y_ref, z_ref, pick_ref, out_ref, picked, half):
+    pick = pick.reshape(2 * lanes, PACK * lanes).astype(jnp.bfloat16)
+    return lane_tiles(y_table), np.stack([lane_tiles(table) for table in z_table]), lane_tiles(pick)
+
+
+def final_body(rows, chunk, modes_ref, feat_ref, kron_ref, bias_ref, y_ref, z_ref, pick_ref, *rest):
+    out_ref, picked, half = rest[-3:]
     plane, part_at = pl.program_id(0), pl.program_id(1)
     channels = feat_ref.shape[0]
     groups = channels // PACK
     length_y = y_ref.shape[1]
     length_z = feat_ref.shape[3] * 16
     lanes = PACK * KZ
+    pairs = PACK // 2
 
     @pl.when(part_at == 0)
     def prepare():
@@ -278,82 +294,107 @@
             high, low = split(jnp.concatenate([real, imag], axis=1))
             stacked += [high, low]
         left = jnp.concatenate(stacked, axis=0)
-        for at in range(0, 2 * PACK, 2):
+        for at in range(0, 2 * pairs, 2):
             value = dot(left, jnp.concatenate([pick_ref[at], pick_ref[at + 1]], axis=1)).astype(BF16)
             picked[at] = value[:, :lanes]
             picked[at + 1] = value[:, lanes:]
-        y_table = wide(y_ref)[:, : 6 * KY]
-        lane = lax.broadcasted_iota(jnp.int32, (length_y // 8, 16, lanes), 2)
+        y_table = wide(y_ref)[:, : 6 * KY + 16]
         for g in range(groups):
             high, low = 2 * g * KY, (2 * g + 1) * KY
-            for pair in range(PACK // 2):
+            for f in range(pairs // 2):
                 parts = [
                     jnp.concatenate(
-                        [picked[s * PACK + 2 * pair + i, h : h + KY, :] for h in (high, low, high) for s in range(2)],
+                        [picked[s * pairs + 2 * f + t, h : h + KY, :] for h in (high, low, high) for s in range(2)]
+                        + [bias_ref[g * pairs + 2 * f + t]],
                         axis=0,
                     )
-                    for i in range(2)
+                    for t in range(2)
                 ]
                 found = dot(y_table, jnp.concatenate(parts, axis=1))
                 found = found.reshape(length_y // 8, 8, 2 * lanes)
                 found = jnp.concatenate([found[:, :, :lanes], found[:, :, lanes:]], axis=1)
                 top = found.astype(BF16)
-                rest = (found - top.astype(F32)).astype(BF16)
-                value = jnp.where(lane // (2 * KZ) == 1, rest, top)
-                first = (g * PACK + 2 * pair) * 8
-                value = jnp.where(lane < 6 * KZ, value, bias_ref[first : first + 16, :][None])
-                half[:, first : first + 16, :] = value
+                first = (g * pairs + 2 * f) * 8
+                half[0, :, first : first + 16, :] = top
+                half[1, :, first : first + 16, :] = (found - top.astype(F32)).astype(BF16)
+
+    kron = wide(kron_ref)
+    z_tables = [wide(z_ref.at[slot]) for slot in range(2)]
+    size = channels * 4
 
     def block(b, carry):
-        feats = rows_of(feat_ref[:, 0, b])
-        h = dot(kron_ref[...], feats) + dot(half[part_at * (chunk // 8) + b], wide(z_ref))
-        inner = h * (h * h * (8.0 * 0.7978845608 * 0.044715) + 2.0 * 0.7978845608)
-        result = h * jnp.tanh(inner) + h
-        result = result.reshape(channels, 8, length_z)
-        parts = [result[:, :, t * 128 : (t + 1) * 128] for t in range(length_z // 128)]
-        out_ref[:, 0, b] = jnp.concatenate(parts, axis=1).astype(BF16)
+        feats = rows_of(feat_ref[:, 0, b]).astype(BF16)
+        at = part_at * (chunk // 8) + b
+        left = jnp.concatenate([half[0, at], half[1, at]], axis=1)
+        for slot in range(2):
+            h = dot(kron[slot * size : (slot + 1) * size], feats) + dot(left, z_tables[slot])
+            inner = h * (h * h * (8.0 * 0.7978845608 * 0.044715) + 2.0 * 0.7978845608)
+            result = (h * jnp.tanh(inner) + h).reshape(channels // 2, 8, length_z)
+            parts = [result[:, :, t * 128 : (t + 1) * 128] for t in range(length_z // 128)]
+            result = jnp.concatenate(parts, axis=1).astype(BF16)
+            for i in range(channels // 2):
+                out_ref[2 * i + slot, 0, b] = result[i]
         return carry
 
-    lax.fori_loop(0, chunk // 8, block, 0, unroll=8)
-
-
-def final(spread, features, pointwise_weight, pointwise_bias, length_x, chunk):
-    channels, planes, length_y, length_z = features.shape
-    rows = 2 * planes
-    groups = channels // PACK
-    lanes = PACK * KZ
-    y_table, z_table, pick = final_tables(length_x, length_y, length_z)
-    kron = jnp.kron(0.5 * pointwise_weight.astype(F32), jnp.eye(8, dtype=F32))
-    tiles = tile_view(features)
-    bias = 0.5 * pointwise_bias
+    lax.fori_loop(0, chunk // 8, block, 0, unroll=UNROLL)
+
+
+def final_operands(features, pointwise_weight, pointwise_bias, length_x):
+    length_y, length_z = features.shape[2:]
+    lanes = PACK * KZ
+    tables = [jnp.asarray(table) for table in final_tables(length_x, length_y, length_z)]
+    channels = features.shape[0]
+    weight = 0.5 * pointwise_weight.astype(F32)
+    weight = weight.reshape(channels // 2, 2, channels).swapaxes(0, 1).reshape(channels, channels)
+    kron = jnp.kron(weight, jnp.eye(8, dtype=F32)).astype(BF16)
+    kron = kron.reshape(channels * 8, channels // 16, 128).swapaxes(0, 1)
+    bias = pointwise_bias * (1.0 * length_x * length_y * length_z)
     b0 = lax.reduce_precision(bias, 8, 7)
     b1 = lax.reduce_precision(bias - b0, 8, 7)
     b2 = bias - b0 - b1
-    pieces = jnp.stack([b0, b1, b2], axis=1)
-    bias_rows = jnp.pad(pieces, ((0, 0), (6 * KZ, lanes - 6 * KZ - 3))).astype(BF16)
-    bias_rows = jnp.repeat(bias_rows, 8, axis=0)
+    pieces = jnp.stack([b0, b1, b2], axis=0).reshape(3, channels // 2, 2).swapaxes(0, 1).astype(BF16)
+    pieces = jnp.pad(pieces[:, :, :, None, None], ((0, 0), (0, 13), (0, 0), (0, 0), (0, 31)))
+    pieces = jnp.broadcast_to(pieces, (channels // 2, 16, 2, 2, 32)).reshape(channels // 2, 16, lanes)
+    return [kron, pieces] + tables
+
+
+def final(spread, tiles, operands, first_plane, count, chunk, before):
+    channels, planes, blocks = tiles.shape[:3]
+    rows = 2 * count
+    groups = channels // PACK
+    lanes = PACK * KZ
 
     def fixed(array):
         return pl.BlockSpec(array.shape, lambda p, q: (0,) * array.ndim)
 
-    tables = [jnp.asarray(y_table), jnp.asarray(z_table), jnp.asarray(pick)]
-    grid_block = pl.BlockSpec((channels, 1, chunk // 8, tiles.shape[3], 128), lambda p, q: (0, p, q, 0, 0))
-    out = pl.pallas_call(
+    grid_block = pl.BlockSpec(
+        (channels, 1, chunk // 8, tiles.shape[3], 128), lambda p, q: (0, p + first_plane, q, 0, 0)
+    )
+    in_specs = [fixed(spread), grid_block] + [fixed(operand) for operand in operands]
+    arguments = [spread, tiles] + operands
+    aliases = {}
+    if before is not None:
+        aliases = {len(arguments): 0}
+        in_specs.append(pl.BlockSpec(memory_space=pl.ANY))
+        arguments.append(before)
+    points = channels * count * blocks * 8 * tiles.shape[3] * 16
+    return pl.pallas_call(
         functools.partial(final_body, rows, chunk),
         out_shape=jax.ShapeDtypeStruct(tiles.shape, BF16),
-        grid=(planes, length_y // chunk),
-        in_specs=[fixed(spread), grid_block, fixed(kron), fixed(bias_rows)] + [fixed(t) for t in tables],
+        grid=(count, blocks * 8 // chunk),
+        in_specs=in_specs,
         out_specs=grid_block,
         scratch_shapes=[
-            pltpu.VMEM((2 * PACK, groups * 2 * KY, lanes), BF16),
-            pltpu.VMEM((length_y // 8, channels * 8, lanes), BF16),
+            pltpu.VMEM((PACK, groups * 2 * KY, lanes), BF16),
+            pltpu.VMEM((2, blocks, channels * 4, lanes), BF16),
         ],
+        input_output_aliases=aliases,
+        cost_estimate=pl.CostEstimate(flops=points * 2000, bytes_accessed=4 * points, transcendentals=points),
         compiler_params=pltpu.CompilerParams(
             dimension_semantics=("arbitrary", "arbitrary"), vmem_limit_bytes=48 << 20
         ),
         name="final_yz",
-    )(spread, tiles, kron, bias_rows, *tables)
-    return from_tile_view(out)
+    )(*arguments)
 
 
 def fused(devices, features, pointwise_weight, pointwise_bias, spectral_weight):
@@ -366,10 +407,23 @@
     shape = (devices, local * groups * rows, lanes)
     partial_value = forward(features, 4).reshape(shape)
     gathered = lax.all_to_all(partial_value, "px", split_axis=0, concat_axis=0)
-    spread = middle(gathered, spectral_weight, length_x, local, groups)
-    spread = lax.all_to_all(spread, "px", split_axis=0, concat_axis=0)
-    spread = spread.reshape(KY * groups * rows, lanes)
-    return final(spread, features, pointwise_weight, pointwise_bias, length_x, 128)
+    parts = 2
+    count = planes // parts
+    spreads = middle(gathered, spectral_weight, length_x, local, groups, parts)
+    tiles = tile_view(features)
+    operands = final_operands(features, pointwise_weight, pointwise_bias, length_x)
+    arrived, out = None, None
+    ready = []
+    for spread in spreads:
+        if arrived is not None:
+            spread, arrived = lax.optimization_barrier((spread, arrived))
+            ready[-1] = arrived
+        arrived = lax.all_to_all(spread, "px", split_axis=0, concat_axis=0)
+        ready.append(arrived)
+    for part, spread in enumerate(ready):
+        spread = spread.reshape(KY * groups * 2 * count, lanes)
+        out = final(spread, tiles, operands, part * count, count, 256, out)
+    return from_tile_view(out)
 
 
 def signed_modes(number):
@@ -489,10 +543,10 @@
     channels, planes, length_y, length_z = features.shape
     fits = (
         KY == 2 * devices
-        and planes % 4 == 0
-        and channels % PACK == 0
+        and planes % 8 == 0
+        and channels == 32
         and length_y % 128 == 0
-        and length_z % 128 == 0
+        and length_z == 256
     )
     call = functools.partial(fused, devices) if fits else functools.partial(plain, planes * devices)
     return call(features, pointwise_weight, pointwise_bias, spectral_weight)

time: 130 us -> 116 us (0.89)
  waiting for transfers between devices: 16 us -> 6.66 us
  Pallas kernels: 65.9 us -> 59.8 us
  starting transfers between devices: 5.02 us -> 9.34 us
    all_to_all x1 -> x2, waiting for transfers between devices: 16 us -> 6.66 us  [fused(): arrived = lax.all_to_all(spread, 'px', split_axis=0, concat_axis=0)]
    pallas_call x1 -> x2, Pallas kernels: 43.4 us -> 36.2 us  [final(): pl.pallas_call(functools.partial(final_body, rows, chunk), out_shape=jax....]
    all_to_all x1 -> x2, starting transfers between devices: 5.02 us -> 9.34 us  [fused(): arrived = lax.all_to_all(spread, 'px', split_axis=0, concat_axis=0)]
    convert_element_type x0 -> x2, local copies, waits for them, and re-layouts: none -> 4.17 us  [final_operands(): kron = jnp.kron(weight, jnp.eye(8, dtype=F32)).astype(BF16)]
    mul x1, local copies, waits for them, and re-layouts: 4.02 us -> 0.07 us  [final_operands(): kron = jnp.kron(weight, jnp.eye(8, dtype=F32)).astype(BF16)]
    unnamed x23 -> x18, local copies, waits for them, and re-layouts: 2.88 us -> 0.04 us
    mul x2 -> x1, other arithmetic: 2.62 us -> 0.01 us  [final_operands(): weight = 0.5 * pointwise_weight.astype(F32)]
    convert_element_type x1 -> x2, other arithmetic: 0.01 us -> 1.73 us  [final_operands(): kron = jnp.kron(weight, jnp.eye(8, dtype=F32)).astype(BF16)]
  transfers between devices with their start and end apart: 1 -> 2, of which waited for: 1 -> 1; matrix products, arithmetic and copies ran while one was open for 5% -> 7% of each run, Pallas kernels for 0% -> 16%
where the time goes in v1:
time: 116 us; the launch traced here: 115 us
  Pallas kernels  59.8 us (52%)
  blocking collectives  31.9 us (28%)
  starting transfers between devices  9.34 us (8%)
  waiting for transfers between devices  6.66 us (6%)
  local copies, waits for them, and re-layouts  5.79 us (5%)
  other arithmetic  1.75 us (2%)
    pallas_call x2, Pallas kernels, final(): pl.pallas_call(functools.partial(final_body, rows, chunk), out_shape=jax....  36.2 us
    all_to_all x1, blocking collectives, fused(): gathered = lax.all_to_all(partial_value, 'px', split_axis=0, concat_axis=0)  31.9 us
    pallas_call x1, Pallas kernels, forward(): pl.pallas_call(functools.partial(forward_body, rows, block_planes), out_s...  18.4 us
    all_to_all x2, starting transfers between devices, fused(): arrived = lax.all_to_all(spread, 'px', split_axis=0, concat_axis=0)  9.34 us
    all_to_all x2, waiting for transfers between devices, fused(): arrived = lax.all_to_all(spread, 'px', split_axis=0, concat_axis=0)  6.66 us
    pallas_call x1, Pallas kernels, middle(): pl.pallas_call(functools.partial(middle_body, local, groups, parts), out_...  5.14 us
    convert_element_type x2, local copies, waits for them, and re-layouts, final_operands(): kron = jnp.kron(weight, jnp.eye(8, dtype=F32)).astype(BF16)  4.17 us
  transfers between devices with their start and end apart: 2, of which 1 were waited for; matrix products, arithmetic and copies ran while one was open for 7% of the time, Pallas kernels for 16%

profile of v1, /device:TPU:0, one launch (start us, length us, event | category | flops | bytes accessed | tf_op | source)
XLA Modules:
  0.0 115.4 jit_solution(7135162609728533340)
XLA Ops:
  0.0 18.4 %forward_zy.1 = f32[2048,128]{1,0:T(8,128)S(1)} custom-call(bf16[32,8,32,16,128]{4,3,2,1,0:T(8,128)(2,1)} %bitcast.35, bf16[8,2,256,128]{3,2,1,0:T(8,128)(2,1)} %constant.21.clone.z_ref, bf16[2,128,128]{2,1,0:T(8,128)(2,1)} %constant.22.clone.y_ref), custom_call_target="tpu_custom_call" | custom-call | tf_op jit(solution)/shard_map/forward_zy/pallas_call | solution.py:120
  18.4 31.9 %all_to_all.15.in_ref = f32[16,128,128]{2,1,0:T(8,128)S(1)} all-to-all(f32[16,128,128]{2,1,0:T(8,128)S(1)} %bitcast.30), channel_id=1, replica_groups=mesh['groups'=2,'px'=16] {'px'}, dimensions={0} | all-to-all | bytes 2097152 | tf_op jit(solution)/shard_map/all_to_all | solution.py:409
  50.3 0.0 copy-start.6
  50.4 0.0 copy-start.5
  50.4 5.1 %middle_x.1 = (f32[16,64,128]{2,1,0:T(8,128)}, f32[16,64,128]{2,1,0:T(8,128)}) custom-call(f32[16,128,128]{2,1,0:T(8,128)S(1)} %all_to_all.15.in_ref, f32[2,32,32,1024]{3,2,1,0:T(8,128)S(1)} %bitcast.29, bf16[2,128,128]{2,1,0:T(8,128)(2,1)S(1)} %copy-done.4, bf16[2,256,128]{2,1,0:T(8,128)(2,1)S(1)} %copy-done.3), custom_call_target="tpu_custom_call" | custom-call | tf_op jit(solution)/shard_map/middle_x/pallas_call | solution.py:234
  55.5 5.2 %all-to-all-start.1 = ((f32[16,64,128]{2,1,0:T(8,128)}), f32[16,64,128]{2,1,0:T(8,128)S(1)}, u32[]{:S(2)}, u32[]{:S(2)}) async-start(f32[16,64,128]{2,1,0:T(8,128)} %get-tuple-element.10), calls=%async_computation.1 | async-start | bytes 1048576 | tf_op jit(solution)/shard_map/all_to_all | solution.py:421
  60.7 0.1 stack.12
  60.8 0.1 copy.27
  60.9 0.1 stack.14
  61.0 0.1 copy.29
  61.1 0.1 stack.13
  61.2 0.1 copy.28
  61.3 0.1 copy.25
  61.4 0.1 pad_bitcast_fusion
  61.6 0.4 copy.30
  61.9 0.3 broadcast_in_dim.16
  62.2 0.2 reshape.64.bias_ref
  62.4 1.7 %multiply_convert_fusion = bf16[32,8,32,8]{1,0,3,2:T(8,128)(2,1)} fusion(f32[8,8]{0,1:T(8,128)S(1)} %fusion, f32[32,32]{0,1:T(8,128)S(1)} %copy.25), kind=kLoop, calls=%fused_computation | loop fusion | flops 131072 | bytes 135424 | tf_op jit(solution)/shard_map/convert_element_type | solution.py:349
  64.1 4.1 %convert_element_type.26 = bf16[256,2,128]{0,2,1:T(8,128)(2,1)S(1)} reshape(bf16[32,8,32,8]{1,0,3,2:T(8,128)(2,1)} %multiply_convert_fusion) | data formatting | bytes 262144 | tf_op jit(solution)/shard_map/convert_element_type | solution.py:349
  68.2 0.1 copy.26
  68.3 6.7 %all-to-all-done.1 = f32[16,64,128]{2,1,0:T(8,128)S(1)} async-done(((f32[16,64,128]{2,1,0:T(8,128)}), f32[16,64,128]{2,1,0:T(8,128)S(1)}, u32[]{:S(2)}, u32[]{:S(2)}) %all-to-all-start.1) | async-done | bytes 524320 | tf_op jit(solution)/shard_map/all_to_all | solution.py:421
  75.0 4.2 %all-to-all-start.2 = ((f32[16,64,128]{2,1,0:T(8,128)}), f32[16,64,128]{2,1,0:T(8,128)S(1)}, u32[]{:S(2)}, u32[]{:S(2)}) async-start(f32[16,64,128]{2,1,0:T(8,128)} %get-tuple-element.11), calls=%async_computation.2 | async-start | bytes 1048576 | tf_op jit(solution)/shard_map/all_to_all | solution.py:421
  79.2 18.1 %final_yz.2.rest_0_ = bf16[32,8,32,16,128]{4,3,2,1,0:T(8,128)(2,1)} custom-call(f32[1024,128]{1,0:T(8,128)S(1)} %bitcast.31, bf16[32,8,32,16,128]{4,3,2,1,0:T(8,128)(2,1)} %bitcast.36, bf16[2,256,128]{2,1,0:T(8,128)(2,1)S(1)} %bitcast.33, bf16[16,16,128]{2,1,0:T(8,128)(2,1)S(1)} %reshape.64.bias_ref, bf16[2,256,128]{2,1,0:T(8,128)(2,1)S(1)} %copy-done.2, ...), custom_call_target="tpu_custom_call" | custom-call | flops 16777216000 | bytes 33554432 | tf_op jit(solution)/shard_map/final_yz/pallas_call | solution.py:381
  97.3 18.1 %final_yz.3 = bf16[32,8,32,16,128]{4,3,2,1,0:T(8,128)(2,1)} custom-call(f32[1024,128]{1,0:T(8,128)S(1)} %bitcast.32, bf16[32,8,32,16,128]{4,3,2,1,0:T(8,128)(2,1)} %bitcast.37, bf16[2,256,128]{2,1,0:T(8,128)(2,1)S(1)} %bitcast.34, bf16[16,16,128]{2,1,0:T(8,128)(2,1)S(1)} %reshape.64.bias_ref, ...), custom_call_target="tpu_custom_call", output_to_operand_aliasing={{}: (7, {})} | custom-call | flops 16777216000 | bytes 33554432 | tf_op jit(solution)/shard_map/final_yz/pallas_call | solution.py:381
  (23 shorter events, 0.1 us)
Async XLA Ops:
  0.0 50.3 %slice-start = ((s8[8388608]{0:T(1024)(128)(4,1)}), s8[4194304]{0:T(1024)(128)(4,1)S(1)}, s32[]{:S(2)}) async-start(s8[8388608]{0:T(1024)(128)(4,1)} %bitcast.28), calls=%async_computation.3 | async-start | bytes 8388608
  0.0 50.3 %slice-start.1 = ((s8[8388608]{0:T(1024)(128)(4,1)}), s8[4194304]{0:T(1024)(128)(4,1)S(1)}, s32[]{:S(2)}) async-start(s8[8388608]{0:T(1024)(128)(4,1)} %bitcast.28), calls=%async_computation.4 | async-start | bytes 8388608
  0.0 50.3 %copy-start.3 = (bf16[2,256,128]{2,1,0:T(8,128)(2,1)S(1)}, bf16[2,256,128]{2,1,0:T(8,128)(2,1)}, u32[]{:S(2)}) copy-start(bf16[2,256,128]{2,1,0:T(8,128)(2,1)} %constant.24.clone.back_ref) | copy-start | bytes 393220
  0.0 50.3 %copy-start.4 = (bf16[2,128,128]{2,1,0:T(8,128)(2,1)S(1)}, bf16[2,128,128]{2,1,0:T(8,128)(2,1)}, u32[]{:S(2)}) copy-start(bf16[2,128,128]{2,1,0:T(8,128)(2,1)} %constant.23.clone.ahead_ref) | copy-start | bytes 196612
  50.3 10.3 %copy-start.6 = (f32[32]{0:T(128)S(1)}, f32[32]{0:T(128)}, u32[]{:S(2)}) copy-start(f32[32]{0:T(128)} %param.13) | copy-start | bytes 388
  50.4 10.9 %copy-start.5 = (bf16[32,32]{1,0:T(8,128)(2,1)S(1)}, bf16[32,32]{1,0:T(8,128)(2,1)}, u32[]{:S(2)}) copy-start(bf16[32,32]{1,0:T(8,128)(2,1)} %param.12) | copy-start | bytes 6148
  55.5 23.6 %copy-start = (bf16[8,256,128]{2,1,0:T(8,128)(2,1)S(1)}, bf16[8,256,128]{2,1,0:T(8,128)(2,1)}, u32[]{:S(2)}) copy-start(bf16[8,256,128]{2,1,0:T(8,128)(2,1)} %constant.27.clone.pick_ref) | copy-start | bytes 1572868
  55.5 23.6 %copy-start.1 = (bf16[2,2,256,128]{3,2,1,0:T(8,128)(2,1)S(1)}, bf16[2,2,256,128]{3,2,1,0:T(8,128)(2,1)}, u32[]{:S(2)}) copy-start(bf16[2,2,256,128]{3,2,1,0:T(8,128)(2,1)} %constant.26.clone.z_ref) | copy-start | bytes 786436
  55.5 23.6 %copy-start.2 = (bf16[2,256,128]{2,1,0:T(8,128)(2,1)S(1)}, bf16[2,256,128]{2,1,0:T(8,128)(2,1)}, u32[]{:S(2)}) copy-start(bf16[2,256,128]{2,1,0:T(8,128)(2,1)} %constant.25.clone.y_ref) | copy-start | bytes 393220
  55.5 19.4 %all-to-all-start.1 = ((f32[16,64,128]{2,1,0:T(8,128)}), f32[16,64,128]{2,1,0:T(8,128)S(1)}, u32[]{:S(2)}, u32[]{:S(2)}) async-start(f32[16,64,128]{2,1,0:T(8,128)} %get-tuple-element.10), calls=%async_computation.1 | async-start | bytes 1048576 | tf_op jit(solution)/shard_map/all_to_all | solution.py:421
  75.0 22.3 %all-to-all-start.2 = ((f32[16,64,128]{2,1,0:T(8,128)}), f32[16,64,128]{2,1,0:T(8,128)S(1)}, u32[]{:S(2)}, u32[]{:S(2)}) async-start(f32[16,64,128]{2,1,0:T(8,128)} %get-tuple-element.11), calls=%async_computation.2 | async-start | bytes 1048576 | tf_op jit(solution)/shard_map/all_to_all | solution.py:421

commit v2 on v1

--- a/solution.py
+++ b/solution.py
@@ -13,7 +13,8 @@
 KY = 32
 KZ = 16
 TWO_PI = 2.0 * math.pi
-UNROLL = 32
+PARTS = 2
+PIECES = 4
 PACK = 8
 F32 = jnp.float32
 BF16 = jnp.bfloat16
@@ -89,50 +90,89 @@
     return z_tables, lane_tiles(np.concatenate([high, low], axis=0))
 
 
-def forward_body(rows, block_planes, feat_ref, z_ref, y_ref, out_ref):
-    plane_at, group_at = pl.program_id(0), pl.program_id(1)
-    groups = pl.num_programs(1)
-    blocks, height = feat_ref.shape[2:4]
+def forward_body(first_plane, block_planes, feat_ref, z_from, y_from, out_ref, held, arrivals, z_ref, y_ref, tables):
+    channels, planes, blocks, height = held.shape[:4]
     length_y = blocks * 8
     lanes = PACK * KZ
-    y_table = wide(y_ref)
-    total = None
-    for j in range(PACK):
-        part = dot(rows_of(feat_ref[j].reshape(block_planes * blocks, height, 128)).astype(BF16), wide(z_ref.at[j]))
-        total = part if total is None else total + part
-    for p in range(block_planes):
-        high, low = split(total[p * length_y : (p + 1) * length_y])
-        first = dot(y_table, high)
-        both = first[: 2 * KY] + first[2 * KY :] + dot(y_table[: 2 * KY], low)
-        cosine, sine = both[:KY], both[KY:]
-        row = group_at * rows + (plane_at * block_planes + p) * 2
-        out_ref[pl.ds(row, KY, stride=groups * rows), :] = cosine[:, :lanes] + sine[:, lanes:]
-        out_ref[pl.ds(row + 1, KY, stride=groups * rows), :] = cosine[:, lanes:] - sine[:, :lanes]
-
-
-def forward(features, block_planes):
-    channels, planes, length_y, length_z = features.shape
     groups = channels // PACK
     rows = 2 * planes
-    lanes = PACK * KZ
-    z_tables, y_tables = forward_tables(length_y, length_z)
-    tiles = tile_view(features)
+    copies = [
+        pltpu.make_async_copy(z_from, z_ref, tables.at[0]),
+        pltpu.make_async_copy(y_from, y_ref, tables.at[1]),
+    ]
+
+    def load(step):
+        across, along = pl.ds((step % groups) * PACK, PACK), (step // groups) * block_planes
+        return pltpu.make_async_copy(
+            feat_ref.at[across, pl.ds(first_plane + along, block_planes)],
+            held.at[across, pl.ds(along, block_planes)],
+            arrivals.at[step],
+        )
+
+    steps = groups * (planes // block_planes)
+    for copy in copies:
+        copy.start()
+    load(0).start()
+    for copy in copies:
+        copy.wait()
+    y_table = wide(y_ref)
+
+    def one(step, carry):
+        group_at, plane_at = step % groups, step // groups
+        load(step).wait()
+
+        @pl.when(step == 0)
+        def second():
+            load(1).start()
+
+        @pl.when(step + 2 < steps)
+        def ahead():
+            load(step + 2).start()
+
+        total = None
+        for j in range(PACK):
+            tiles = held[group_at * PACK + j, pl.ds(plane_at * block_planes, block_planes)]
+            left = rows_of(tiles.reshape(block_planes * blocks, height, 128)).astype(BF16)
+            part = dot(left, wide(z_ref.at[j]))
+            total = part if total is None else total + part
+        for p in range(block_planes):
+            high, low = split(total[p * length_y : (p + 1) * length_y])
+            first = dot(y_table, high)
+            both = first[: 2 * KY] + first[2 * KY :] + dot(y_table[: 2 * KY], low)
+            cosine, sine = both[:KY], both[KY:]
+            row = group_at * rows + (plane_at * block_planes + p) * 2
+            out_ref[pl.ds(row, KY, stride=groups * rows), :] = cosine[:, :lanes] + sine[:, lanes:]
+            out_ref[pl.ds(row + 1, KY, stride=groups * rows), :] = cosine[:, lanes:] - sine[:, :lanes]
+        return carry
+
+    lax.fori_loop(0, steps, one, 0)
+
+
+def forward(tiles, first_plane, planes, block_planes):
+    channels, _, blocks, height = tiles.shape[:4]
+    groups = channels // PACK
+    lanes = PACK * KZ
+    z_tables, y_tables = forward_tables(blocks * 8, height * 16)
+    steps = groups * (planes // block_planes)
+    whole = pl.BlockSpec(memory_space=pltpu.VMEM)
+    points = channels * planes * blocks * 8 * height * 16
     return pl.pallas_call(
-        functools.partial(forward_body, rows, block_planes),
-        out_shape=jax.ShapeDtypeStruct((KY * groups * rows, lanes), F32),
-        grid=(planes // block_planes, groups),
-        in_specs=[
-            pl.BlockSpec((PACK, block_planes) + tiles.shape[2:], lambda p, g: (g, p, 0, 0, 0)),
-            pl.BlockSpec(z_tables.shape, lambda p, g: (0, 0, 0, 0)),
-            pl.BlockSpec(y_tables.shape, lambda p, g: (0, 0, 0)),
+        functools.partial(forward_body, first_plane, block_planes),
+        out_shape=jax.ShapeDtypeStruct((KY * groups * 2 * planes, lanes), F32),
+        in_specs=[pl.BlockSpec(memory_space=pltpu.HBM)] * 3,
+        out_specs=whole,
+        scratch_shapes=[
+            pltpu.VMEM((channels, planes) + tiles.shape[2:], BF16),
+            pltpu.SemaphoreType.DMA((steps,)),
+            pltpu.VMEM(z_tables.shape, BF16),
+            pltpu.VMEM(y_tables.shape, BF16),
+            pltpu.SemaphoreType.DMA((2,)),
         ],
-        out_specs=pl.BlockSpec((KY * groups * rows, lanes), lambda p, g: (0, 0)),
-        compiler_params=pltpu.CompilerParams(
-            dimension_semantics=("arbitrary", "arbitrary"), vmem_limit_bytes=40 << 20
-        ),
+        cost_estimate=pl.CostEstimate(flops=points * 1000, bytes_accessed=2 * points, transcendentals=0),
+        compiler_params=pltpu.CompilerParams(vmem_limit_bytes=44 << 20),
         name="forward_zy",
     )(
-        tiles,
+        pltpu.with_memory_space_constraint(tiles, pltpu.HBM),
         pltpu.with_memory_space_constraint(jnp.asarray(z_tables), pltpu.HBM),
         pltpu.with_memory_space_constraint(jnp.asarray(y_tables), pltpu.HBM),
     )
@@ -170,10 +210,19 @@
     return results
 
 
-def middle_body(local, groups, parts, in_ref, weight_ref, ahead_ref, back_ref, *rest):
-    out_refs, (turned, spec, mixed) = rest[:parts], rest[parts:]
+def middle_body(local, groups, parts, in_ref, weight_ref, ahead_ref, back_ref, *refs):
+    out_refs, (turned, spec, mixed, weights, arrivals) = refs[:parts], refs[parts:]
+    weight_tiles = weights.shape[0]
+
+    def load(tile):
+        here = pl.ds(pl.multiple_of(tile * 128, 128), 128)
+        return pltpu.make_async_copy(weight_ref.at[:, :, :, here], weights.at[tile], arrivals.at[tile])
+
+    for tile in range(weight_tiles):
+        load(tile).start()
     devices, _, lanes = in_ref.shape
     rows = in_ref.shape[1] // (local * groups)
+    size = rows // parts
     channels = groups * PACK
     quarter = KZ // 4
     tables = wide(ahead_ref)
@@ -194,10 +243,11 @@
 
     def mix(tile, carry):
         here = pl.ds(pl.multiple_of(tile * 128, 128), 128)
+        load(tile).wait()
         real = imag = None
         for i in range(channels):
             s_real, s_imag = spec[0, i : i + 1, here], spec[1, i : i + 1, here]
-            w_real, w_imag = weight_ref[0, i, :, here], weight_ref[1, i, :, here]
+            w_real, w_imag = weights[tile, 0, i], weights[tile, 1, i]
             add_real = s_real * w_real - s_imag * w_imag
             add_imag = s_real * w_imag + s_imag * w_real
             real = add_real if real is None else real + add_real
@@ -206,7 +256,7 @@
         mixed[1, :, here] = imag
         return carry
 
-    lax.fori_loop(0, local * quarter, mix, 0)
+    lax.fori_loop(0, weight_tiles, mix, 0)
     for g in range(groups):
         for t in range(quarter):
             pieces = [
@@ -220,7 +270,6 @@
             high, low = split(modes[k * 2 * KX : (k + 1) * 2 * KX])
             spread = dot(back_table, jnp.concatenate([high, low, high], axis=0))
             spread = spread.reshape(devices, rows, lanes)
-            size = rows // parts
             at = (k * groups + g) * size
             for part, out_ref in enumerate(out_refs):
                 out_ref[:, at : at + size, :] = spread[:, part * size : (part + 1) * size]
@@ -228,22 +277,30 @@
 
 def middle(gathered, spectral_weight, length_x, local, groups, parts):
     channels = spectral_weight.shape[1]
+    devices, height, lanes = gathered.shape
     ahead, back = middle_tables(length_x)
     modes = spectral_weight.shape[3]
     whole = pl.BlockSpec(memory_space=pltpu.VMEM)
     return pl.pallas_call(
         functools.partial(middle_body, local, groups, parts),
-        out_shape=[jax.ShapeDtypeStruct((gathered.shape[0], gathered.shape[1] // parts, gathered.shape[2]), F32)] * parts,
-        in_specs=[whole] * 4,
+        out_shape=[jax.ShapeDtypeStruct((devices, height // parts, lanes), F32)] * parts,
+        in_specs=[whole, pl.BlockSpec(memory_space=pltpu.HBM), whole, whole],
         out_specs=[whole] * parts,
         scratch_shapes=[
             pltpu.VMEM((PACK * KZ, local * 2 * KX), F32),
             pltpu.VMEM((2, channels, modes), F32),
             pltpu.VMEM((2, channels, modes), F32),
+            pltpu.VMEM((modes // 128, 2, channels, channels, 128), F32),
+            pltpu.SemaphoreType.DMA((modes // 128,)),
         ],
         compiler_params=pltpu.CompilerParams(vmem_limit_bytes=32 << 20),
         name="middle_x",
-    )(gathered, spectral_weight, jnp.asarray(ahead), jnp.asarray(back))
+    )(
+        gathered,
+        pltpu.with_memory_space_constraint(spectral_weight, pltpu.HBM),
+        jnp.asarray(ahead),
+        jnp.asarray(back),
+    )
 
 
 def final_tables(length_x, length_y, length_z):
@@ -274,9 +331,22 @@
     return lane_tiles(y_table), np.stack([lane_tiles(table) for table in z_table]), lane_tiles(pick)
 
 
-def final_body(rows, chunk, modes_ref, feat_ref, kron_ref, bias_ref, y_ref, z_ref, pick_ref, *rest):
-    out_ref, picked, half = rest[-3:]
-    plane, part_at = pl.program_id(0), pl.program_id(1)
+def final_body(rows, first_plane, modes_ref, feat_ref, kron_ref, bias_ref, y_ref, z_ref, pick_ref, *rest):
+    out_ref, picked, half, feats_in, results, arrivals, departures = rest[-7:]
+    count, _, blocks = feats_in.shape[:3]
+    span = blocks // PIECES
+
+    def load(plane):
+        return pltpu.make_async_copy(feat_ref.at[:, first_plane + plane], feats_in.at[plane], arrivals.at[plane])
+
+    def leave(plane, piece):
+        slot = plane % 2
+        at = pl.ds(piece * span, span)
+        return pltpu.make_async_copy(
+            results.at[slot, :, at], out_ref.at[:, first_plane + plane, at], departures.at[slot, piece]
+        )
+
+    load(0).start()
     channels = feat_ref.shape[0]
     groups = channels // PACK
     length_y = y_ref.shape[1]
@@ -284,8 +354,7 @@
     lanes = PACK * KZ
     pairs = PACK // 2
 
-    @pl.when(part_at == 0)
-    def prepare():
+    def prepare(plane):
         stacked = []
         for g in range(groups):
             row = g * rows + plane * 2
@@ -322,21 +391,44 @@
     z_tables = [wide(z_ref.at[slot]) for slot in range(2)]
     size = channels * 4
 
-    def block(b, carry):
-        feats = rows_of(feat_ref[:, 0, b]).astype(BF16)
-        at = part_at * (chunk // 8) + b
-        left = jnp.concatenate([half[0, at], half[1, at]], axis=1)
-        for slot in range(2):
-            h = dot(kron[slot * size : (slot + 1) * size], feats) + dot(left, z_tables[slot])
-            inner = h * (h * h * (8.0 * 0.7978845608 * 0.044715) + 2.0 * 0.7978845608)
-            result = (h * jnp.tanh(inner) + h).reshape(channels // 2, 8, length_z)
-            parts = [result[:, :, t * 128 : (t + 1) * 128] for t in range(length_z // 128)]
-            result = jnp.concatenate(parts, axis=1).astype(BF16)
-            for i in range(channels // 2):
-                out_ref[2 * i + slot, 0, b] = result[i]
+    def one(plane, carry):
+        slot = plane % 2
+
+        @pl.when(plane >= 2)
+        def drain():
+            for piece in range(PIECES):
+                leave(plane - 2, piece).wait()
+
+        prepare(plane)
+        load(plane).wait()
+
+        @pl.when(plane == 0)
+        def second():
+            load(1).start()
+
+        @pl.when(plane + 2 < count)
+        def ahead():
+            load(plane + 2).start()
+
+        for b in range(blocks):
+            feats = rows_of(feats_in[plane, :, b]).astype(BF16)
+            left = jnp.concatenate([half[0, b], half[1, b]], axis=1)
+            for side in range(2):
+                h = dot(kron[side * size : (side + 1) * size], feats) + dot(left, z_tables[side])
+                inner = h * (h * h * (8.0 * 0.7978845608 * 0.044715) + 2.0 * 0.7978845608)
+                result = (h * jnp.tanh(inner) + h).reshape(channels // 2, 8, length_z)
+                parts = [result[:, :, t * 128 : (t + 1) * 128] for t in range(length_z // 128)]
+                result = jnp.concatenate(parts, axis=1).astype(BF16)
+                for i in range(channels // 2):
+                    results[slot, 2 * i + side, b] = result[i]
+            if (b + 1) % span == 0:
+                leave(plane, b // span).start()
         return carry
 
-    lax.fori_loop(0, chunk // 8, block, 0, unroll=UNROLL)
+    lax.fori_loop(0, count, one, 0)
+    for plane in range(max(count - 2, 0), count):
+        for piece in range(PIECES):
+            leave(plane, piece).wait()
 
 
 def final_operands(features, pointwise_weight, pointwise_bias, length_x):
@@ -358,43 +450,48 @@
     return [kron, pieces] + tables
 
 
-def final(spread, tiles, operands, first_plane, count, chunk, before):
-    channels, planes, blocks = tiles.shape[:3]
+def final(spread, tiles, operands, first_plane, count, before):
+    channels, planes, blocks, height = tiles.shape[:4]
     rows = 2 * count
     groups = channels // PACK
     lanes = PACK * KZ
-
-    def fixed(array):
-        return pl.BlockSpec(array.shape, lambda p, q: (0,) * array.ndim)
-
-    grid_block = pl.BlockSpec(
-        (channels, 1, chunk // 8, tiles.shape[3], 128), lambda p, q: (0, p + first_plane, q, 0, 0)
-    )
-    in_specs = [fixed(spread), grid_block] + [fixed(operand) for operand in operands]
+    whole = pl.BlockSpec(memory_space=pltpu.VMEM)
+    apart = pl.BlockSpec(memory_space=pltpu.HBM)
+    in_specs = [whole, apart] + [whole] * len(operands)
     arguments = [spread, tiles] + operands
     aliases = {}
     if before is not None:
         aliases = {len(arguments): 0}
-        in_specs.append(pl.BlockSpec(memory_space=pl.ANY))
+        in_specs.append(apart)
         arguments.append(before)
-    points = channels * count * blocks * 8 * tiles.shape[3] * 16
+    points = channels * count * blocks * 8 * height * 16
     return pl.pallas_call(
-        functools.partial(final_body, rows, chunk),
+        functools.partial(final_body, rows, first_plane),
         out_shape=jax.ShapeDtypeStruct(tiles.shape, BF16),
-        grid=(count, blocks * 8 // chunk),
         in_specs=in_specs,
-        out_specs=grid_block,
+        out_specs=apart,
         scratch_shapes=[
             pltpu.VMEM((PACK, groups * 2 * KY, lanes), BF16),
             pltpu.VMEM((2, blocks, channels * 4, lanes), BF16),
+            pltpu.VMEM((count, channels, blocks, height, 128), BF16),
+            pltpu.VMEM((2, channels, blocks, height, 128), BF16),
+            pltpu.SemaphoreType.DMA((count,)),
+            pltpu.SemaphoreType.DMA((2, PIECES)),
         ],
         input_output_aliases=aliases,
         cost_estimate=pl.CostEstimate(flops=points * 2000, bytes_accessed=4 * points, transcendentals=points),
-        compiler_params=pltpu.CompilerParams(
-            dimension_semantics=("arbitrary", "arbitrary"), vmem_limit_bytes=48 << 20
-        ),
+        compiler_params=pltpu.CompilerParams(vmem_limit_bytes=40 << 20),
         name="final_yz",
     )(*arguments)
+
+
+def exchange(values):
+    arrived = []
+    for value in values:
+        if arrived:
+            value, arrived[-1] = lax.optimization_barrier((value, arrived[-1]))
+        arrived.append(lax.all_to_all(value, "px", split_axis=0, concat_axis=0))
+    return arrived
 
 
 def fused(devices, features, pointwise_weight, pointwise_bias, spectral_weight):
@@ -402,27 +499,22 @@
     length_x = planes * devices
     local = KY // devices
     groups = channels // PACK
-    rows = 2 * planes
-    lanes = PACK * KZ
-    shape = (devices, local * groups * rows, lanes)
-    partial_value = forward(features, 4).reshape(shape)
+    lanes = PACK * KZ
+    count = planes // PARTS
+    shape = (devices, local * groups * 2 * planes, lanes)
+    tiles = tile_view(features)
+    partial_value = forward(tiles, 0, planes, 4).reshape(shape)
+    partial_value, pointwise_weight, pointwise_bias = lax.optimization_barrier(
+        (partial_value, pointwise_weight, pointwise_bias)
+    )
+    operands = final_operands(features, pointwise_weight, pointwise_bias, length_x)
     gathered = lax.all_to_all(partial_value, "px", split_axis=0, concat_axis=0)
-    parts = 2
-    count = planes // parts
-    spreads = middle(gathered, spectral_weight, length_x, local, groups, parts)
-    tiles = tile_view(features)
-    operands = final_operands(features, pointwise_weight, pointwise_bias, length_x)
-    arrived, out = None, None
-    ready = []
-    for spread in spreads:
-        if arrived is not None:
-            spread, arrived = lax.optimization_barrier((spread, arrived))
-            ready[-1] = arrived
-        arrived = lax.all_to_all(spread, "px", split_axis=0, concat_axis=0)
-        ready.append(arrived)
-    for part, spread in enumerate(ready):
+    gathered, operands[0], operands[1] = lax.optimization_barrier((gathered, operands[0], operands[1]))
+    spreads = middle(gathered, spectral_weight, length_x, local, groups, PARTS)
+    out = None
+    for part, spread in enumerate(exchange(spreads)):
         spread = spread.reshape(KY * groups * 2 * count, lanes)
-        out = final(spread, tiles, operands, part * count, count, 256, out)
+        out = final(spread, tiles, operands, part * count, count, out)
     return from_tile_view(out)
 
 
@@ -545,6 +637,7 @@
         KY == 2 * devices
         and planes % 8 == 0
         and channels == 32
+        and planes * length_y * length_z <= 1 << 19
         and length_y % 128 == 0
         and length_z == 256
     )

time: 116 us -> 113 us (0.974)
  waiting for transfers between devices: 6.66 us -> 17.8 us
  blocking collectives: 31.9 us -> 20.9 us
  Pallas kernels: 59.8 us -> 56.6 us
  starting transfers between devices: 9.34 us -> 11.7 us
  other arithmetic: 1.75 us -> 0.43 us
  local copies, waits for them, and re-layouts: 5.79 us -> 4.59 us
    all_to_all x2, waiting for transfers between devices: 6.66 us -> 17.8 us  [the longest x1 17.8 us: fused(): gathered = lax.all_to_all(partial_value, 'px', split_axis=0, concat_axis=0)]
    all_to_all x1, blocking collectives: 31.9 us -> 20.9 us  [exchange(): arrived.append(lax.all_to_all(value, 'px', split_axis=0, concat_axis=0))]
    pallas_call x3, Pallas kernels: 54.6 us -> 50.9 us  [the longest x2 33.9 us: final(): pl.pallas_call(functools.partial(final_body, rows, first_plane), out_shap...]
    all_to_all x2, starting transfers between devices: 9.34 us -> 11.7 us  [the longest x1 7.52 us: fused(): gathered = lax.all_to_all(partial_value, 'px', split_axis=0, concat_axis=0)]
    convert_element_type x2, other arithmetic: 1.73 us -> 0.41 us  [final_operands(): kron = jnp.kron(weight, jnp.eye(8, dtype=F32)).astype(BF16)]
    convert_element_type x2, local copies, waits for them, and re-layouts: 4.17 us -> 2.98 us  [final_operands(): kron = jnp.kron(weight, jnp.eye(8, dtype=F32)).astype(BF16)]
  transfers between devices with their start and end apart: 2 -> 2, of which waited for: 1 -> 1; matrix products, arithmetic and copies ran while one was open for 7% -> 4% of each run, Pallas kernels for 16% -> 15%
where the time goes in v2:
time: 113 us; the launch traced here: 112 us
  Pallas kernels  56.6 us (50%)
  blocking collectives  20.9 us (18%)
  waiting for transfers between devices  17.8 us (16%)
  starting transfers between devices  11.7 us (10%)
  local copies, waits for them, and re-layouts  4.59 us (4%)
    pallas_call x2, Pallas kernels, final(): pl.pallas_call(functools.partial(final_body, rows, first_plane), out_shap...  33.9 us
    all_to_all x1, blocking collectives, exchange(): arrived.append(lax.all_to_all(value, 'px', split_axis=0, concat_axis=0))  20.9 us
    all_to_all x1, waiting for transfers between devices, fused(): gathered = lax.all_to_all(partial_value, 'px', split_axis=0, concat_axis=0)  17.8 us
    pallas_call x1, Pallas kernels, forward(): pl.pallas_call(functools.partial(forward_body, first_plane, block_planes)...  17 us
    all_to_all x1, starting transfers between devices, fused(): gathered = lax.all_to_all(partial_value, 'px', split_axis=0, concat_axis=0)  7.52 us
    pallas_call x1, Pallas kernels, middle(): pl.pallas_call(functools.partial(middle_body, local, groups, parts), out_...  5.74 us
    all_to_all x1, starting transfers between devices, exchange(): arrived.append(lax.all_to_all(value, 'px', split_axis=0, concat_axis=0))  4.17 us
    convert_element_type x2, local copies, waits for them, and re-layouts, final_operands(): kron = jnp.kron(weight, jnp.eye(8, dtype=F32)).astype(BF16)  2.98 us
  transfers between devices with their start and end apart: 2, of which 1 were waited for; matrix products, arithmetic and copies ran while one was open for 4% of the time, Pallas kernels for 15%

profile of v2, /device:TPU:0, one launch (start us, length us, event | category | flops | bytes accessed | tf_op | source)
XLA Modules:
  0.0 112.4 jit_solution(8949804939717699681)
XLA Ops:
  0.0 17.0 %forward_zy.1 = f32[2048,128]{1,0:T(8,128)} custom-call(bf16[32,8,32,16,128]{4,3,2,1,0:T(8,128)(2,1)} %bitcast.32, bf16[8,2,256,128]{3,2,1,0:T(8,128)(2,1)} %constant.21.clone.z_from, bf16[2,128,128]{2,1,0:T(8,128)(2,1)} %constant.22.clone.y_from), custom_call_target="tpu_custom_call" | custom-call | flops 16777216000 | bytes 33554432 | tf_op jit(solution)/shard_map/forward_zy/pallas_call | solution.py:159
  17.0 0.0 copy-start.3
  17.0 0.0 copy-start.4
  17.0 7.5 %all-to-all-start = ((f32[16,128,128]{2,1,0:T(8,128)}), f32[16,128,128]{2,1,0:T(8,128)S(1)}, u32[]{:S(2)}, u32[]{:S(2)}) async-start(f32[16,128,128]{2,1,0:T(8,128)} %bitcast.3), calls=%async_computation | async-start | bytes 2097152 | tf_op jit(solution)/shard_map/all_to_all | solution.py:511
  24.6 0.1 stack.12
  24.6 0.1 copy.27
  24.7 0.1 stack.14
  24.8 0.1 copy.29
  24.9 0.1 stack.13
  25.0 0.1 copy.28
  25.2 0.1 copy.25
  25.3 0.1 pad_bitcast_fusion
  25.4 0.4 copy.30
  25.8 0.3 broadcast_in_dim.16
  26.0 0.2 reshape.61.bias_ref
  26.2 0.4 multiply_convert_fusion
  26.6 2.9 %convert_element_type.26 = bf16[256,2,128]{0,2,1:T(8,128)(2,1)S(1)} reshape(bf16[32,8,32,8]{1,0,3,2:T(8,128)(2,1)S(1)} %multiply_convert_fusion) | data formatting | bytes 262144 | tf_op jit(solution)/shard_map/convert_element_type | solution.py:441
  29.5 0.1 copy.26
  29.6 17.8 %all-to-all-done.in_ref = f32[16,128,128]{2,1,0:T(8,128)S(1)} async-done(((f32[16,128,128]{2,1,0:T(8,128)}), f32[16,128,128]{2,1,0:T(8,128)S(1)}, u32[]{:S(2)}, u32[]{:S(2)}) %all-to-all-start) | async-done | bytes 1048608 | tf_op jit(solution)/shard_map/all_to_all | solution.py:511
  47.4 5.7 %middle_x.1 = (f32[16,64,128]{2,1,0:T(8,128)S(1)}, f32[16,64,128]{2,1,0:T(8,128)}) custom-call(f32[16,128,128]{2,1,0:T(8,128)S(1)} %all-to-all-done.in_ref, f32[2,32,32,1024]{3,2,1,0:T(8,128)} %weight_ref.1, bf16[2,128,128]{2,1,0:T(8,128)(2,1)S(1)} %copy-done.4, bf16[2,256,128]{2,1,0:T(8,128)(2,1)S(1)} %copy-done.3), custom_call_target="tpu_custom_call" | custom-call | tf_op jit(solution)/shard_map/middle_x/pallas_call | solution.py:284
  53.2 20.9 %all_to_all.15 = f32[16,64,128]{2,1,0:T(8,128)S(1)} all-to-all(f32[16,64,128]{2,1,0:T(8,128)S(1)} %get-tuple-element.20), channel_id=1, replica_groups=mesh['groups'=2,'px'=16] {'px'}, dimensions={0} | all-to-all | bytes 1048576 | tf_op jit(solution)/shard_map/all_to_all | solution.py:493
  74.1 4.2 %all-to-all-start.2 = ((f32[16,64,128]{2,1,0:T(8,128)}), f32[16,64,128]{2,1,0:T(8,128)S(1)}, u32[]{:S(2)}, u32[]{:S(2)}) async-start(f32[16,64,128]{2,1,0:T(8,128)} %get-tuple-element.21), calls=%async_computation.2 | async-start | bytes 1048576 | tf_op jit(solution)/shard_map/all_to_all | solution.py:493
  78.3 17.0 %final_yz.2.rest_0_ = bf16[32,8,32,16,128]{4,3,2,1,0:T(8,128)(2,1)} custom-call(f32[1024,128]{1,0:T(8,128)S(1)} %bitcast.29, bf16[32,8,32,16,128]{4,3,2,1,0:T(8,128)(2,1)} %bitcast.33, bf16[2,256,128]{2,1,0:T(8,128)(2,1)S(1)} %bitcast.30, bf16[16,16,128]{2,1,0:T(8,128)(2,1)S(1)} %reshape.61.bias_ref, bf16[2,256,128]{2,1,0:T(8,128)(2,1)S(1)} %copy-done.2, ...), custom_call_target="tpu_custom_call" | custom-call | flops 16777216000 | bytes 33554432 | tf_op jit(solution)/shard_map/final_yz/pallas_call | solution.py:468
  95.3 17.0 %final_yz.3 = bf16[32,8,32,16,128]{4,3,2,1,0:T(8,128)(2,1)} custom-call(f32[1024,128]{1,0:T(8,128)S(1)} %bitcast.28, bf16[32,8,32,16,128]{4,3,2,1,0:T(8,128)(2,1)} %bitcast.34, bf16[2,256,128]{2,1,0:T(8,128)(2,1)S(1)} %bitcast.31, bf16[16,16,128]{2,1,0:T(8,128)(2,1)S(1)} %reshape.61.bias_ref, ...), custom_call_target="tpu_custom_call", output_to_operand_aliasing={{}: (7, {})} | custom-call | flops 16777216000 | bytes 33554432 | tf_op jit(solution)/shard_map/final_yz/pallas_call | solution.py:468
  (18 shorter events, 0.1 us)
Async XLA Ops:
  0.0 24.5 %copy-start.6 = (f32[32]{0:T(128)S(1)}, f32[32]{0:T(128)}, u32[]{:S(2)}) copy-start(f32[32]{0:T(128)} %param.13) | copy-start | bytes 388
  0.0 25.1 %copy-start.5 = (bf16[32,32]{1,0:T(8,128)(2,1)S(1)}, bf16[32,32]{1,0:T(8,128)(2,1)}, u32[]{:S(2)}) copy-start(bf16[32,32]{1,0:T(8,128)(2,1)} %param.12) | copy-start | bytes 6148
  17.0 30.4 %copy-start.3 = (bf16[2,256,128]{2,1,0:T(8,128)(2,1)S(1)}, bf16[2,256,128]{2,1,0:T(8,128)(2,1)}, u32[]{:S(2)}) copy-start(bf16[2,256,128]{2,1,0:T(8,128)(2,1)} %constant.27.clone.back_ref) | copy-start | bytes 393220
  17.0 30.4 %copy-start.4 = (bf16[2,128,128]{2,1,0:T(8,128)(2,1)S(1)}, bf16[2,128,128]{2,1,0:T(8,128)(2,1)}, u32[]{:S(2)}) copy-start(bf16[2,128,128]{2,1,0:T(8,128)(2,1)} %constant.26.clone.ahead_ref) | copy-start | bytes 196612
  17.0 30.4 %all-to-all-start = ((f32[16,128,128]{2,1,0:T(8,128)}), f32[16,128,128]{2,1,0:T(8,128)S(1)}, u32[]{:S(2)}, u32[]{:S(2)}) async-start(f32[16,128,128]{2,1,0:T(8,128)} %bitcast.3), calls=%async_computation | async-start | bytes 2097152 | tf_op jit(solution)/shard_map/all_to_all | solution.py:511
  47.4 30.8 %copy-start = (bf16[8,256,128]{2,1,0:T(8,128)(2,1)S(1)}, bf16[8,256,128]{2,1,0:T(8,128)(2,1)}, u32[]{:S(2)}) copy-start(bf16[8,256,128]{2,1,0:T(8,128)(2,1)} %constant.25.clone.pick_ref) | copy-start | bytes 1572868
  47.4 30.8 %copy-start.1 = (bf16[2,2,256,128]{3,2,1,0:T(8,128)(2,1)S(1)}, bf16[2,2,256,128]{3,2,1,0:T(8,128)(2,1)}, u32[]{:S(2)}) copy-start(bf16[2,2,256,128]{3,2,1,0:T(8,128)(2,1)} %constant.24.clone.z_ref) | copy-start | bytes 786436
  47.4 30.8 %copy-start.2 = (bf16[2,256,128]{2,1,0:T(8,128)(2,1)S(1)}, bf16[2,256,128]{2,1,0:T(8,128)(2,1)}, u32[]{:S(2)}) copy-start(bf16[2,256,128]{2,1,0:T(8,128)(2,1)} %constant.23.clone.y_ref) | copy-start | bytes 393220
  74.1 21.2 %all-to-all-start.2 = ((f32[16,64,128]{2,1,0:T(8,128)}), f32[16,64,128]{2,1,0:T(8,128)S(1)}, u32[]{:S(2)}, u32[]{:S(2)}) async-start(f32[16,64,128]{2,1,0:T(8,128)} %get-tuple-element.21), calls=%async_computation.2 | async-start | bytes 1048576 | tf_op jit(solution)/shard_map/all_to_all | solution.py:493
